TPU v7x, 32 devices: a whole 2x2x4 slice. The times are simulated.
32 devices in a mesh: part: 2 (over x), col: 4 (over z), row: 4 (over y, core).
Axes of the slice: x: 2, y: 2, z: 4, core: 2. Of those that a mesh axis runs over, the one named last changes fastest.
Arguments:
- a_blocks: float32 [80, 128, 5120], P(('part', 'row'), None, 'col'), parts along dimension 0
Outputs:
- output: float32 [80, 128, 5120], P(('part', 'row'), None, 'col'), parts along dimension 0
There are 2 independent parts. A program takes and returns all parts, laid end to end along the dimension named above; each array names one.
All inputs are finite; a program needn't handle non-finite values.
Results may differ from a plain program's by a relative error of at most 0.001.
Values sent between devices are 32-bit elements.
A program may use at most 1 GiB of HBM per device.

v0:
```python
import jax
import jax.numpy as jnp
from jax import lax
from jax.sharding import PartitionSpec as P

FULL_PRECISION = lax.Precision.HIGHEST


def solution(mesh):
    grid_rows = mesh.shape["row"]
    grid_cols = mesh.shape["col"]

    def local_factor(blocks):
        row_blocks, block_size, local_cols = blocks.shape
        col_blocks = local_cols // block_size
        num_blocks = row_blocks * grid_rows
        my_row = lax.axis_index("row")
        my_col = lax.axis_index("col")
        for k_step in range(num_blocks):
            owner_row = k_step % grid_rows
            owner_col = k_step % grid_cols
            diag_tile = k_step // grid_rows
            diag_lo = (k_step // grid_cols) * block_size
            diag_hi = diag_lo + block_size
            on_row = my_row == owner_row
            on_col = my_col == owner_col
            diag_local = blocks[diag_tile, :, diag_lo:diag_hi]
            diag_sum = lax.psum(jnp.where(on_row, diag_local, 0.0), "row")
            diag_fac = jnp.linalg.cholesky(diag_sum)
            blocks = blocks.at[diag_tile, :, diag_lo:diag_hi].set(jnp.where(on_row & on_col, diag_fac, diag_local))
            row_lo = (k_step + 1) // grid_rows
            if row_lo < row_blocks:
                col_lo = (k_step + 1) // grid_cols
                trail_rows = row_blocks - row_lo
                panel_in = blocks[row_lo:, :, diag_lo:diag_hi]
                solved = lax.linalg.triangular_solve(diag_fac, panel_in.reshape(trail_rows * block_size, block_size), left_side=False, lower=True, transpose_a=True)
                glob_rows = (row_lo + jnp.arange(trail_rows)) * grid_rows + my_row
                keep_rows = (glob_rows > k_step)[:, None, None]
                row_panel = lax.psum(jnp.where(keep_rows & on_col, solved.reshape(trail_rows, block_size, block_size), 0.0), "col")
                blocks = blocks.at[row_lo:, :, diag_lo:diag_hi].set(jnp.where(keep_rows & on_col, row_panel, panel_in))
                gathered = lax.all_gather(row_panel, "row", axis=1).reshape(trail_rows * grid_rows, block_size, block_size)
                padded = jnp.concatenate([jnp.zeros((row_lo * grid_rows, block_size, block_size), blocks.dtype), gathered], axis=0)
                col_panel = lax.dynamic_index_in_dim(padded.reshape(col_blocks, grid_cols, block_size, block_size), my_col, axis=1, keepdims=False)[col_lo:]
                update = lax.dot_general(row_panel.reshape(trail_rows * block_size, block_size), col_panel.reshape((col_blocks - col_lo) * block_size, block_size), (((1,), (1,)), ((), ())), precision=FULL_PRECISION, preferred_element_type=jnp.float32)
                trail_old = blocks[row_lo:, :, col_lo * block_size:]
                blocks = blocks.at[row_lo:, :, col_lo * block_size:].set(trail_old - update.reshape(trail_old.shape))
        shaped = blocks.reshape(row_blocks, block_size, col_blocks, block_size)
        glob_row_ids = (jnp.arange(row_blocks) * grid_rows + my_row)[:, None, None, None]
        glob_col_ids = (jnp.arange(col_blocks) * grid_cols + my_col)[None, None, :, None]
        inner_row = jnp.arange(block_size)[None, :, None, None]
        inner_col = jnp.arange(block_size)[None, None, None, :]
        lower_part = (glob_row_ids > glob_col_ids) | ((glob_row_ids == glob_col_ids) & (inner_row >= inner_col))
        return jnp.where(lower_part, shaped, 0.0).reshape(row_blocks, block_size, local_cols)

    block_spec = P(("part", "row"), None, "col")
    return jax.shard_map(local_factor, mesh=mesh, in_specs=(block_spec,), out_specs=block_spec, check_vma=False)
```

profile of v0, /device:TPU:0, one launch (start us, length us, event | category | flops | bytes accessed | tf_op | source)
XLA Modules:
  0.0 4913.2 jit_solution(4530464089210803868)
XLA Ops:
  80.5 40.8 all-reduce.118.cloned.1.call-done
  227.0 40.4 all-reduce.122.cloned.1.call-done
  372.5 40.8 all-reduce.126.cloned.1.call-done
  518.7 39.8 all-reduce.130.cloned.1.call-done
  658.7 40.0 all-reduce.134.cloned.1.call-done
  798.8 40.0 all-reduce.138.cloned.1.call-done
  939.0 40.0 all-reduce.142.cloned.1.call-done
  1079.2 38.7 all-reduce.146.cloned.1.call-done
  1215.0 38.7 all-reduce.150.cloned.1.call-done
  1350.9 38.7 all-reduce.154.cloned.1.call-done
  1486.9 38.7 all-reduce.158.cloned.1.call-done
  1622.7 37.9 all-reduce.162.cloned.1.call-done
  1754.6 37.9 all-reduce.166.cloned.1.call-done
  1886.5 37.9 all-reduce.170.cloned.1.call-done
  2018.6 37.9 all-reduce.174.cloned.1.call-done
  2150.3 37.1 all-reduce.178.cloned.1.call-done
  2279.2 37.1 all-reduce.182.cloned.1.call-done
  2408.3 37.1 all-reduce.186.cloned.1.call-done
  2537.4 37.1 all-reduce.190.cloned.1.call-done
  2666.5 36.5 all-reduce.194.cloned.1.call-done
  2790.2 36.5 all-reduce.198.cloned.1.call-done
  2913.8 36.5 all-reduce.202.cloned.1.call-done
  3037.4 36.5 all-reduce.206.cloned.1.call-done
  3398.7 35.6 all-reduce.218.cloned.1.call-done
  (1313 shorter events, 3975.7 us)
Async XLA Ops:
  16.1 105.2 %all-reduce.118.cloned.1.call-start = ((), (), s32[]{:S(2)}) async-start(), calls=%async_computation.1 | async-start | bytes 1310720 | tf_op jit(solution)/shard_map/psum | solution.py:39
  164.9 102.5 %all-reduce.122.cloned.1.call-start = ((), (), s32[]{:S(2)}) async-start(), calls=%async_computation.3 | async-start | bytes 1310720 | tf_op jit(solution)/shard_map/psum | solution.py:39
  310.8 102.5 %all-reduce.126.cloned.1.call-start = ((), (), s32[]{:S(2)}) async-start(), calls=%async_computation.5 | async-start | bytes 1310720 | tf_op jit(solution)/shard_map/psum | solution.py:39
  456.9 101.6 %all-reduce.130.cloned.1.call-start = ((), (), s32[]{:S(2)}) async-start(), calls=%async_computation.7 | async-start | bytes 1179648 | tf_op jit(solution)/shard_map/psum | solution.py:39
  596.5 102.2 %all-reduce.134.cloned.1.call-start = ((), (), s32[]{:S(2)}) async-start(), calls=%async_computation.9 | async-start | bytes 1179648 | tf_op jit(solution)/shard_map/psum | solution.py:39
  736.7 102.2 %all-reduce.138.cloned.1.call-start = ((), (), s32[]{:S(2)}) async-start(), calls=%async_computation.11 | async-start | bytes 1179648 | tf_op jit(solution)/shard_map/psum | solution.py:39
  876.9 102.2 %all-reduce.142.cloned.1.call-start = ((), (), s32[]{:S(2)}) async-start(), calls=%async_computation.13 | async-start | bytes 1179648 | tf_op jit(solution)/shard_map/psum | solution.py:39
  1017.2 100.6 %all-reduce.146.cloned.1.call-start = ((), (), s32[]{:S(2)}) async-start(), calls=%async_computation.15 | async-start | bytes 1048576 | tf_op jit(solution)/shard_map/psum | solution.py:39
  1153.1 100.6 %all-reduce.150.cloned.1.call-start = ((), (), s32[]{:S(2)}) async-start(), calls=%async_computation.17 | async-start | bytes 1048576 | tf_op jit(solution)/shard_map/psum | solution.py:39
  1289.0 100.7 %all-reduce.154.cloned.1.call-start = ((), (), s32[]{:S(2)}) async-start(), calls=%async_computation.19 | async-start | bytes 1048576 | tf_op jit(solution)/shard_map/psum | solution.py:39
  1424.9 100.6 %all-reduce.158.cloned.1.call-start = ((), (), s32[]{:S(2)}) async-start(), calls=%async_computation.21 | async-start | bytes 1048576 | tf_op jit(solution)/shard_map/psum | solution.py:39
  1560.8 99.7 %all-reduce.162.cloned.1.call-start = ((), (), s32[]{:S(2)}) async-start(), calls=%async_computation.23 | async-start | bytes 917504 | tf_op jit(solution)/shard_map/psum | solution.py:39
  1692.9 99.6 %all-reduce.166.cloned.1.call-start = ((), (), s32[]{:S(2)}) async-start(), calls=%async_computation.25 | async-start | bytes 917504 | tf_op jit(solution)/shard_map/psum | solution.py:39
  1824.8 99.6 %all-reduce.170.cloned.1.call-start = ((), (), s32[]{:S(2)}) async-start(), calls=%async_computation.27 | async-start | bytes 917504 | tf_op jit(solution)/shard_map/psum | solution.py:39
  1956.9 99.6 %all-reduce.174.cloned.1.call-start = ((), (), s32[]{:S(2)}) async-start(), calls=%async_computation.29 | async-start | bytes 917504 | tf_op jit(solution)/shard_map/psum | solution.py:39
  2088.8 98.5 %all-reduce.178.cloned.1.call-start = ((), (), s32[]{:S(2)}) async-start(), calls=%async_computation.31 | async-start | bytes 786432 | tf_op jit(solution)/shard_map/psum | solution.py:39
  2217.8 98.6 %all-reduce.182.cloned.1.call-start = ((), (), s32[]{:S(2)}) async-start(), calls=%async_computation.33 | async-start | bytes 786432 | tf_op jit(solution)/shard_map/psum | solution.py:39
  2346.8 98.6 %all-reduce.186.cloned.1.call-start = ((), (), s32[]{:S(2)}) async-start(), calls=%async_computation.35 | async-start | bytes 786432 | tf_op jit(solution)/shard_map/psum | solution.py:39
  2475.9 98.6 %all-reduce.190.cloned.1.call-start = ((), (), s32[]{:S(2)}) async-start(), calls=%async_computation.37 | async-start | bytes 786432 | tf_op jit(solution)/shard_map/psum | solution.py:39
  2605.1 97.9 %all-reduce.194.cloned.1.call-start = ((), (), s32[]{:S(2)}) async-start(), calls=%async_computation.39 | async-start | bytes 655360 | tf_op jit(solution)/shard_map/psum | solution.py:39
  2729.3 97.4 %all-reduce.198.cloned.1.call-start = ((), (), s32[]{:S(2)}) async-start(), calls=%async_computation.41 | async-start | bytes 655360 | tf_op jit(solution)/shard_map/psum | solution.py:39
  2852.9 97.4 %all-reduce.202.cloned.1.call-start = ((), (), s32[]{:S(2)}) async-start(), calls=%async_computation.43 | async-start | bytes 655360 | tf_op jit(solution)/shard_map/psum | solution.py:39
  2976.5 97.4 %all-reduce.206.cloned.1.call-start = ((), (), s32[]{:S(2)}) async-start(), calls=%async_computation.45 | async-start | bytes 655360 | tf_op jit(solution)/shard_map/psum | solution.py:39
  3338.0 96.3 %all-reduce.218.cloned.1.call-start = ((), (), s32[]{:S(2)}) async-start(), calls=%async_computation.51 | async-start | bytes 524288 | tf_op jit(solution)/shard_map/psum | solution.py:39
  (132 other events, 6483.5 us)
Sparse Core Ops, SparseCore 0:
  80.6 40.7 all-reduce.117
  226.7 40.7 all-reduce.121
  372.6 40.7 all-reduce.125
  518.5 39.9 all-reduce.129
  658.7 39.9 all-reduce.133
  798.9 39.9 all-reduce.137
  939.1 39.9 all-reduce.141
  1079.2 38.5 all-reduce.145
  1215.1 38.5 all-reduce.149
  1351.0 38.6 all-reduce.153
  1486.9 38.5 all-reduce.157
  1622.8 37.7 all-reduce.161
  1754.7 37.7 all-reduce.165
  1886.6 37.7 all-reduce.169
  2018.7 37.7 all-reduce.173
  2150.3 36.9 all-reduce.177
  2279.3 36.9 all-reduce.181
  2408.3 36.9 all-reduce.185
  2537.5 36.9 all-reduce.189
  2666.6 36.3 all-reduce.193
  2790.3 36.4 all-reduce.197
  2913.9 36.3 all-reduce.201
  3037.5 36.4 all-reduce.205
  3398.8 35.4 all-reduce.217
  (82 shorter events, 2324.8 us)
where the time goes:
time: 4930 us; the launch traced here: 4910 us
  waiting for transfers between devices  3210 us (65%)
  other arithmetic  1140 us (23%)
  local copies, waits for them, and re-layouts  245 us (5%)
  matrix products  191 us (4%)
  blocking collectives  86.5 us (2%)
    psum x39, waiting for transfers between devices, local_factor(): lax.psum(jnp.where(keep_rows & on_col, solved.reshape(trail_rows, block_s...  1440 us
    psum x40, waiting for transfers between devices, local_factor(): diag_sum = lax.psum(jnp.where(on_row, diag_local, 0.0), 'row')  1240 us
    all_gather x27, waiting for transfers between devices, local_factor(): lax.all_gather(row_panel, 'row', axis=1)  537 us
    another operation x120, other arithmetic, local_factor(): diag_fac = jnp.linalg.cholesky(diag_sum)  501 us
    another operation x78, other arithmetic, local_factor(): lax.linalg.triangular_solve(diag_fac, panel_in.reshape(trail_rows * block...  408 us
    dot_general x39, matrix products, local_factor(): lax.dot_general(row_panel.reshape(trail_rows * block_size, block_size), c...  168 us
  transfers between devices with their start and end apart: 106, of which 106 were waited for; matrix products, arithmetic and copies ran while one was open for 1% of the time, Pallas kernels for 0%

commit v1 on v0

v1 whole, which is shorter than its diff:
```python
import jax
import jax.numpy as jnp
from jax import lax
from jax.experimental import pallas as pl
from jax.experimental.pallas import tpu as pltpu
from jax.sharding import PartitionSpec as P

HI = lax.Precision.HIGHEST
MESH = pl.DeviceIdType.MESH
NB = 128
N_STEPS = 40
G = 4
PAIRS = 5
N_BLOCKS = 120


def _factor(s_val, u_ref, w_ref):
    sub = lax.broadcasted_iota(jnp.int32, (8, NB), 0)
    lane = lax.broadcasted_iota(jnp.int32, (8, NB), 1)
    rows = [s_val[8 * t:8 * t + 8, :] for t in range(16)]
    inv = [jnp.where(lane == sub + 8 * t, 1.0, 0.0) for t in range(16)]
    full = (8, NB)
    for b in range(16):
        p, q = rows[b], inv[b]
        ncol = 8 if b == 15 else 16
        cols = [jnp.broadcast_to(p[:, 8 * b + i:8 * b + i + 1], full) for i in range(ncol)]
        for j in range(8):
            rinv = lax.rsqrt(jnp.broadcast_to(cols[j][j:j + 1, :], full))
            low = jnp.where(sub > j, cols[j] * rinv, 0.0)
            prow = jnp.broadcast_to(p[j:j + 1, :], full) * rinv
            p = jnp.where(sub == j, prow, p - low * prow)
            qrow = jnp.broadcast_to(q[j:j + 1, :], full) * rinv
            q = jnp.where(sub == j, qrow, q - low * qrow)
            for i in range(j + 1, ncol):
                crow = jnp.broadcast_to(cols[i][j:j + 1, :], full) * rinv
                nxt = cols[i] - low * crow
                cols[i] = jnp.where(sub == j, crow, nxt) if i >= 8 else nxt
        u_ref[8 * b:8 * b + 8, :] = jnp.where(lane >= sub + 8 * b, p, 0.0)
        w_ref[8 * b:8 * b + 8, :] = q
        if b < 15:
            pn, qn = rows[b + 1], inv[b + 1]
            for i in range(8):
                dp = jnp.sum(cols[8 + i] * p, axis=0, keepdims=True)
                dq = jnp.sum(cols[8 + i] * q, axis=0, keepdims=True)
                pn = jnp.where(sub == i, pn - dp, pn)
                qn = jnp.where(sub == i, qn - dq, qn)
            rows[b + 1], inv[b + 1] = pn, qn
        if b < 14:
            both = jnp.concatenate([p, q], axis=1)
            upd = lax.dot_general(p, both, (((0,), (0,)), ((), ())), precision=HI, preferred_element_type=jnp.float32)
            for t in range(b + 2, 16):
                rows[t] = rows[t] - upd[8 * t:8 * t + 8, :NB]
                inv[t] = inv[t] - upd[8 * t:8 * t + 8, NB:]


def _nt(x, y):
    return lax.dot_general(x, y, (((1,), (1,)), ((), ())), precision=HI, preferred_element_type=jnp.float32)


def _div(x, n):
    return lax.div(x, jnp.int32(n))


def _rem(x, n):
    return lax.rem(x, jnp.int32(n))


def _kernel(a_hbm, o_hbm, mat, pan, wb, raw, diag, ubuf, zero,
            row_sem, col_sem, w_sem, raw_sem, send_sem, in_sem, out_sem):
    me_c = lax.axis_index("col").astype(jnp.int32)
    me_r = lax.axis_index("row").astype(jnp.int32)
    on_diag = me_r == me_c
    side = jnp.where(on_diag, 0, 1).astype(jnp.int32)
    nxt_r, nxt_c = _rem(me_r + 1, G), _rem(me_c + 1, G)
    prv_r, prv_c = _rem(me_r + 3, G), _rem(me_c + 3, G)

    loads = [pltpu.make_async_copy(a_hbm.at[:, :, pl.ds(p * 2 * NB, 2 * NB)], mat.at[p], in_sem.at[p]) for p in range(PAIRS)]
    for cp in loads:
        cp.start()
    zero[...] = jnp.zeros_like(zero)

    barrier = pltpu.get_barrier_semaphore()
    for d in range(1, G):
        pl.semaphore_signal(barrier, inc=1, device_id={"row": _rem(me_r + d, G)}, device_id_type=MESH)
        pl.semaphore_signal(barrier, inc=1, device_id={"col": _rem(me_c + d, G)}, device_id_type=MESH)

    @pl.when(on_diag)
    def _():
        pl.semaphore_signal(barrier, inc=1, device_id={"row": nxt_r, "col": nxt_c}, device_id_type=MESH)
        pl.semaphore_signal(barrier, inc=1, device_id={"row": prv_r, "col": prv_c}, device_id_type=MESH)
    pl.semaphore_wait(barrier, jnp.where(on_diag, 8, 6).astype(jnp.int32))
    for cp in loads:
        cp.wait()

    def index(k, q):
        s = _div(k, 8)
        return 40 * s - 4 * s * (s - 1) + (k - 8 * s) * (5 - s) + (q - s)

    def first(k, x):
        s = _div(k, 8)
        return s + jnp.where(8 * s + 4 + x <= k, 1, 0).astype(jnp.int32)

    def half_of(k):
        return pl.multiple_of(_rem(_div(k, 4), 2) * NB, NB)

    def row_copy(k, q, d):
        blk = pan.at[0, index(k, q)]
        return pltpu.make_async_remote_copy(blk, blk, send_sem.at[0], row_sem.at[index(k, q)],
                                            device_id={"col": _rem(me_c + d, G)}, device_id_type=MESH)

    def col_copy(k, q, d):
        i = index(k, q)
        return pltpu.make_async_remote_copy(pan.at[0, i], pan.at[1, i], send_sem.at[1], col_sem.at[i],
                                            device_id={"row": _rem(me_r + d, G)}, device_id_type=MESH)

    def w_copy(k, d):
        return pltpu.make_async_remote_copy(wb.at[k], wb.at[k], send_sem.at[2], w_sem.at[k],
                                            device_id={"row": _rem(me_r + d, G)}, device_id_type=MESH)

    def w_next_copy(k):
        return pltpu.make_async_remote_copy(wb.at[k], wb.at[k], send_sem.at[2], w_sem.at[k],
                                            device_id={"row": nxt_r, "col": nxt_c}, device_id_type=MESH)

    def raw_copy(k):
        src = mat.at[_div(k, 8), _div(k + 1, 4), :, pl.ds(half_of(k), NB)]
        return pltpu.make_async_remote_copy(src, raw.at[k], send_sem.at[3], raw_sem.at[k],
                                            device_id={"col": nxt_c}, device_id_type=MESH)

    def factor_step(k, with_prev):
        @pl.when((me_r == _rem(k, G)) & (me_c == _rem(k, G)))
        def _():
            t = _div(k, 4)
            blk = mat[_div(k, 8), t, :, pl.ds(half_of(k), NB)]
            if with_prev:
                w_next_copy(k - 1).wait_recv()
                raw_copy(k - 1).wait_recv()
                x = _nt(raw[k - 1], wb[k - 1])
                blk = blk - _nt(x, x)
            _factor(blk, ubuf, wb.at[k])

            @pl.when(k < N_STEPS - 1)
            def _():
                w_next_copy(k).start()
                for d in range(1, G):
                    w_copy(k, d).start()
            diag[t] = ubuf[...].T

    def raw_step(k):
        @pl.when((me_c == _rem(k, G)) & (me_r == _rem(k + 1, G)) & (k < N_STEPS - 1))
        def _():
            raw_copy(k).start()

    def panel_step(k):
        @pl.when(me_c == _rem(k, G))
        def _():
            s = _div(k, 8)
            t = _div(k, 4)

            @pl.when((me_r != _rem(k, G)) & (k < N_STEPS - 1))
            def _():
                w_copy(k, 1).wait_recv()

            def block(q, _):
                i = index(k, q)
                a = mat[s, pl.ds(2 * q, 2), :, pl.ds(half_of(k), NB)].reshape(2 * NB, NB)
                pan[0, i] = _nt(a, wb[k])
                for d in range(1, G):
                    row_copy(k, q, d).start()
                return 0
            lax.fori_loop(jnp.where(k < N_STEPS - 1, first(k, me_r), PAIRS), PAIRS, block, 0)

            def tile(ti, _):
                dst = o_hbm.at[ti, :, pl.ds(pl.multiple_of(t * NB, NB), NB)]
                i = 4 * ti + me_r

                @pl.when(i > k)
                def _():
                    src = pan.at[0, index(k, _div(ti, 2)), pl.ds(pl.multiple_of(_rem(ti, 2) * NB, NB), NB), :]
                    pltpu.make_async_copy(src, dst, out_sem).start()

                @pl.when(i == k)
                def _():
                    pltpu.make_async_copy(diag.at[t], dst, out_sem).start()

                @pl.when(i < k)
                def _():
                    pltpu.make_async_copy(zero, dst, out_sem).start()
                return 0
            lax.fori_loop(0, 10, tile, 0)

    def receive_step(k):
        def row_wait(q, _):
            @pl.when(me_c != _rem(k, G))
            def _():
                row_copy(k, q, 1).wait_recv()

            @pl.when(on_diag)
            def _():
                for d in range(1, G):
                    col_copy(k, q, d).start()
            return 0
        lax.fori_loop(first(k, me_r), PAIRS, row_wait, 0)

        @pl.when(jnp.logical_not(on_diag))
        def _():
            def col_wait(q, _):
                col_copy(k, q, 1).wait_recv()
                return 0
            lax.fori_loop(first(k, me_c), PAIRS, col_wait, 0)

    def update(k, p, _):
        right = pan[side, index(k, p)]

        def rows(q, _):
            rs = pl.ds(2 * q, 2)
            prod = _nt(pan[0, index(k, q)], right)
            mat[p, rs] = mat[p, rs] - prod.reshape(2, NB, 2 * NB)
            return 0
        lax.fori_loop(jnp.maximum(p, first(k, me_r)), PAIRS, rows, 0)
        return 0

    raw_step(jnp.int32(0))
    factor_step(jnp.int32(0), False)
    panel_step(jnp.int32(0))

    def step(k, _):
        factor_step(k + 1, True)

        @pl.when((me_c == _rem(k, G)) & (me_r == _rem(k + 1, G)))
        def _():
            raw_copy(k).wait_send()
        receive_step(k)
        next_col = me_c == _rem(k + 1, G)
        p1 = jnp.where(next_col, _div(k + 1, 8), first(k, me_c))

        @pl.when(next_col)
        def _():
            update(k, p1, 0)
        raw_step(k + 1)
        panel_step(k + 1)
        lax.fori_loop(jnp.where(next_col, p1 + 1, p1), PAIRS, lambda p, x: update(k, p, x), 0)
        return 0
    lax.fori_loop(0, N_STEPS - 1, step, 0)

    def drain(k, _):
        mine = me_c == _rem(k, G)

        @pl.when(mine & (me_r == _rem(k, G)))
        def _():
            for d in range(G):
                w_next_copy(k).wait_send()

        def rows(q, _):
            @pl.when(mine)
            def _():
                for d in range(1, G):
                    row_copy(k, q, d).wait_send()

            @pl.when(on_diag)
            def _():
                for d in range(1, G):
                    col_copy(k, q, d).wait_send()
            return 0
        lax.fori_loop(first(k, me_r), PAIRS, rows, 0)
        return 0
    lax.fori_loop(0, N_STEPS - 1, drain, 0)
    pltpu.make_async_copy(o_hbm, o_hbm, out_sem).wait()


def solution(mesh):
    def local(a):
        return pl.pallas_call(
            _kernel,
            out_shape=jax.ShapeDtypeStruct(a.shape, a.dtype),
            in_specs=[pl.BlockSpec(memory_space=pl.ANY)],
            out_specs=pl.BlockSpec(memory_space=pl.ANY),
            scratch_shapes=[
                pltpu.VMEM((PAIRS, 10, NB, 2 * NB), jnp.float32),
                pltpu.VMEM((2, N_BLOCKS, 2 * NB, NB), jnp.float32),
                pltpu.VMEM((N_STEPS, NB, NB), jnp.float32),
                pltpu.VMEM((N_STEPS, NB, NB), jnp.float32),
                pltpu.VMEM((10, NB, NB), jnp.float32),
                pltpu.VMEM((NB, NB), jnp.float32),
                pltpu.VMEM((NB, NB), jnp.float32),
                pltpu.SemaphoreType.DMA((N_BLOCKS,)),
                pltpu.SemaphoreType.DMA((N_BLOCKS,)),
                pltpu.SemaphoreType.DMA((N_STEPS,)),
                pltpu.SemaphoreType.DMA((N_STEPS,)),
                pltpu.SemaphoreType.DMA((4,)),
                pltpu.SemaphoreType.DMA((PAIRS,)),
                pltpu.SemaphoreType.DMA,
            ],
            compiler_params=pltpu.CompilerParams(collective_id=0, has_side_effects=True, vmem_limit_bytes=63 * 1024 * 1024),
            name="cholesky",
        )(a)

    spec = P(("part", "row"), None, "col")
    return jax.shard_map(local, mesh=mesh, in_specs=(spec,), out_specs=spec, check_vma=False)
```

time: 4930 us -> 950 us (0.19)
  the two profiles are of different devices: /device:TPU:0 before, /device:TPU:27 now
where the time goes in v1:
time: 950 us
  Pallas kernels  944 us (99%)
    pallas_call x1, Pallas kernels, local(): pl.pallas_call(_kernel, out_shape=jax.ShapeDtypeStruct(a.shape, a.dtype),...  944 us

profile of v1, /device:TPU:27, one launch (start us, length us, event | category | flops | bytes accessed | tf_op | source)
XLA Modules:
  0.0 950.0 jit_solution(6596770138708734049)
XLA Ops:
  0.0 943.8 %cholesky.1 = f32[10,128,1280]{2,1,0:T(8,128)} custom-call(f32[10,128,1280]{2,1,0:T(8,128)} %a_hbm.1), custom_call_target="tpu_custom_call" | custom-call | tf_op jit(solution)/shard_map/cholesky/pallas_call | solution.py:272
  943.8 6.2 copy.3
